TPU v7x, 32 devices: a whole 2x2x4 slice. The times are simulated.
32 devices in a mesh: ga: 2 (over core), band: 16 (over z, y, x).
Axes of the slice: x: 2, y: 2, z: 4, core: 2. Of those that a mesh axis runs over, the one named last changes fastest.
Arguments:
- orbitals: bfloat16 [1024, 2, 16384], P('band', None, 'ga'), may hold values from -6 to 6
- projectors: bfloat16 [864, 2, 16384], P(None, None, ('ga', 'band')), may hold values from -0.03125 to 0.03125
- coupling: float32 [4, 18, 18], replicated, may hold values from -6 to 6
- species: int32 [48], replicated, may hold values from 0 to 3
- offsets: int32 [48], replicated, may hold values from 0 to 846, as said below
Outputs:
- applied: bfloat16 [1024, 2, 16384], P('band', None, 'ga')
Inputs may be any that keep to these rules, and one draw needn't show every extreme that they name: Each atom's 18 projectors are the 18 consecutive rows of projectors starting at its offset; offsets are multiples of 18, and the atoms' blocks are distinct and cover all 864 rows.
All inputs are finite; a program needn't handle non-finite values.
Results may differ from a plain program's by a relative error of at most 0.0049.
Values may be sent and summed in bfloat16 or wider, within the bound.
A program may use at most 64 MiB of HBM per device.

v0:
```python
import jax
import jax.numpy as jnp
from jax import lax
from jax.sharding import PartitionSpec as P


def block_matrices(coupling, species, offsets):
    per_atom = coupling.shape[1]
    count = offsets.shape[0]
    blocks = jnp.arange(count, dtype=jnp.int32)
    matches = (offsets[None, :] == blocks[:, None] * per_atom).astype(jnp.int32)
    atom_kind = jnp.sum(matches * species[None, :], axis=1)
    onehot = (atom_kind[:, None] == jnp.arange(coupling.shape[0], dtype=jnp.int32)[None, :]).astype(
        jnp.float32
    )
    table = coupling.reshape(coupling.shape[0], per_atom * per_atom)
    picked = jnp.dot(
        onehot, table, precision=lax.Precision.HIGHEST, preferred_element_type=jnp.float32
    )
    return picked.reshape(count, per_atom, per_atom)


def apply_coupling(matrices, becp):
    count = matrices.shape[0]
    per_atom = matrices.shape[1]
    height = becp.shape[0]
    widths = becp.shape[2]
    blocked = becp.reshape(count, per_atom, 2 * widths)
    coupled = jnp.einsum("aij,ajc->aic", matrices, blocked, precision=lax.Precision.HIGHEST)
    return coupled.reshape(height, 2, widths).astype(jnp.bfloat16)


def project_bands(projectors, spread):
    total_proj = projectors.shape[0]
    total_bands = spread.shape[0]
    flat_proj = projectors.reshape(total_proj, -1)
    turned = jnp.concatenate([spread[:, 1, :], -spread[:, 0, :]], axis=1)
    stacked = jnp.concatenate([spread.reshape(total_bands, -1), turned], axis=0)
    partial_value = lax.dot_general(
        flat_proj, stacked, (((1,), (1,)), ((), ())), preferred_element_type=jnp.float32
    )
    return partial_value.reshape(total_proj, 2, total_bands)


def add_back(projectors, dbecp):
    total_proj = projectors.shape[0]
    total_bands = dbecp.shape[2]
    columns = dbecp.reshape(total_proj, 2 * total_bands)
    real_part = lax.dot_general(
        columns, projectors[:, 0, :], (((0,), (0,)), ((), ())), preferred_element_type=jnp.float32
    )
    imag_part = lax.dot_general(
        columns, projectors[:, 1, :], (((0,), (0,)), ((), ())), preferred_element_type=jnp.float32
    )
    out_real = real_part[:total_bands] - imag_part[total_bands:]
    out_imag = imag_part[:total_bands] + real_part[total_bands:]
    return jnp.stack([out_real, out_imag], axis=1).astype(jnp.bfloat16)


def per_device(orbitals, projectors, coupling, species, offsets):
    matrices = block_matrices(coupling, species, offsets)
    spread = lax.all_to_all(orbitals, "band", split_axis=2, concat_axis=0, tiled=True)
    partial_value = project_bands(projectors, spread)
    becp = lax.psum(partial_value, ("ga", "band"))
    dbecp = apply_coupling(matrices, becp)
    result = add_back(projectors, dbecp)
    return lax.all_to_all(result, "band", split_axis=0, concat_axis=2, tiled=True)


def solution(mesh):
    placed = (P("band", None, "ga"), P(None, None, ("ga", "band")), P(), P(), P())
    return jax.shard_map(
        per_device, mesh=mesh, in_specs=placed, out_specs=P("band", None, "ga"), check_vma=False
    )
```

profile of v0, /device:TPU:0, one launch (start us, length us, event | category | flops | bytes accessed | tf_op | source)
XLA Modules:
  0.0 417.0 jit_solution(8911082358564989493)
XLA Ops:
  6.5 11.4 %copy.45 = bf16[64,2,8192]{0,1,2:T(2,128)(2,1)} copy(bf16[64,2,8192]{2,1,0:T(2,128)(2,1)} %param.5) | data formatting | bytes 4194304 | tf_op args[0]
  17.9 7.5 %reshape.39 = bf16[16,2,32768]{2,1,0:T(2,128)(2,1)} reshape(bf16[8192,2,64]{2,1,0:T(2,128)(2,1)} %bitcast.46) | data formatting | bytes 4194304
  25.4 0.0 copy-start
  25.4 8.5 %all-to-all-start = ((bf16[16,2,32768]{2,1,0:T(2,128)(2,1)}), bf16[16,2,32768]{2,1,0:T(2,128)(2,1)}, u32[]{:S(2)}, u32[]{:S(2)}) async-start(bf16[16,2,32768]{2,1,0:T(2,128)(2,1)} %reshape.39), calls=%async_computation | async-start | bytes 4194304 | tf_op jit(solution)/shard_map/all_to_all | solution.py:62
  34.0 0.0 all-reduce.2.cloned.1.call-start
  34.0 0.0 copy-done
  34.0 0.5 copy.60
  34.5 42.6 %all-to-all-done = bf16[16,2,32768]{2,1,0:T(2,128)(2,1)} async-done(((bf16[16,2,32768]{2,1,0:T(2,128)(2,1)}), bf16[16,2,32768]{2,1,0:T(2,128)(2,1)}, u32[]{:S(2)}, u32[]{:S(2)}) %all-to-all-start) | async-done | bytes 2097184 | tf_op jit(solution)/shard_map/all_to_all | solution.py:62
  77.1 7.4 %reshape.40 = bf16[8192,2,64]{2,1,0:T(2,128)(2,1)} reshape(bf16[16,2,32768]{2,1,0:T(2,128)(2,1)} %all-to-all-done) | data formatting | bytes 4194304
  84.4 10.6 %copy.55 = bf16[64,2,16,512]{3,0,2,1:T(8,128)(2,1)} copy(bf16[64,2,16,512]{0,1,3,2:T(2,128)(2,1)} %bitcast.44) | data formatting | bytes 4194304 | tf_op jit(solution)/shard_map/all_to_all | solution.py:62
  95.0 7.4 %copy.54 = bf16[64,2,16,512]{3,2,0,1:T(8,128)(2,1)} copy(bf16[64,2,16,512]{0,1,3,2:T(2,128)(2,1)} %bitcast.45) | data formatting | bytes 4194304 | tf_op jit(solution)/shard_map/all_to_all | solution.py:62
  102.4 0.0 copy-start.1
  102.4 1.8 slice_bitcast_fusion
  104.2 0.4 copy-done.1
  104.6 2.2 copy.47
  106.8 0.6 copy.59
  107.4 12.5 %fusion.6 = f32[864,2048]{1,0:T(8,128)} fusion(bf16[864,1024]{1,0:T(8,128)(2,1)S(1)} %bitcast.53, bf16[1024,512]{1,0:T(8,128)(2,1)S(1)} %get-tuple-element.8, bf16[1024,512]{1,0:T(8,128)(2,1)S(1)} %get-tuple-element.7, bf16[1024,1024]{1,0:T(8,128)(2,1)S(1)} %bitcast.52), kind=kOutput, calls=%fused_computation.6 | convolution fusion | flops 3636461568 | bytes 13041664 | tf_op jit(solution)/shard_map/dot_general | solution.py:39
  119.9 7.9 %reshape.36 = f32[48,18,2048]{2,1,0:T(8,128)} reshape(f32[864,2048]{1,0:T(8,128)} %fusion.6) | data formatting | bytes 14155776 | tf_op jit(solution)/shard_map/reshape | solution.py:28
  127.8 0.0 copy-start.5
  127.8 0.0 copy-start.6
  127.8 0.0 copy-start.7
  127.8 0.0 all-reduce.2.cloned.1.call-update
  127.8 0.7 copy-done.5
  128.6 0.1 reshape.32
  128.6 0.1 dot_general.22
  128.8 0.0 copy-done.6
  128.8 0.0 copy-done.7
  128.8 0.2 select_reduce_fusion
  128.9 0.4 fusion.16
  129.4 0.3 copy.49
  129.7 4.2 %fusion.22 = (bf16[864,1,512]{2,1,0:T(2,128)(2,1)}, bf16[864,1,512]{2,1,0:T(2,128)(2,1)}) fusion(bf16[864,2,512]{2,1,0:T(2,128)(2,1)S(1)} %copy-done), kind=kLoop, calls=%fused_computation.30 | loop fusion | bytes 3538944 | tf_op jit(solution)/shard_map/slice | solution.py:53
  133.9 189.5 %all-reduce.2.cloned.1.call-done = f32[48,18,2048]{2,1,0:T(8,128)} async-done(((f32[48,18,2048]{2,1,0:T(8,128)}), f32[48,18,2048]{2,1,0:T(8,128)}) %all-reduce.2.cloned.1.call-update) | async-done | bytes 7077904 | tf_op jit(solution)/shard_map/psum | solution.py:64
  323.4 12.2 %convolution_convert_fusion = bf16[48,18,2048]{2,1,0:T(8,128)(2,1)} fusion(f32[48,18,18]{2,1,0:T(8,128)S(1)} %copy.49, f32[48,18,2048]{2,1,0:T(8,128)} %all-reduce.2.cloned.1.call-done), kind=kOutput, calls=%fused_computation.7 | convolution fusion | flops 383975424 | bytes 10679040 | tf_op jit(solution)/shard_map/aij,ajc->aic/dot_general | solution.py:29
  335.5 0.0 copy-start.4
  335.5 6.2 %convert_element_type.12 = bf16[864,2048]{1,0:T(8,128)(2,1)} reshape(bf16[48,18,2048]{2,1,0:T(8,128)(2,1)} %convolution_convert_fusion) | data formatting | bytes 7077888 | tf_op jit(solution)/shard_map/convert_element_type | solution.py:30
  341.7 0.0 copy-done.4
  341.7 0.0 copy-start.2
  341.7 0.0 copy-start.3
  341.8 4.6 %fusion.14 = f32[2048,512]{1,0:T(8,128)S(1)} fusion(bf16[864,2048]{1,0:T(8,128)(2,1)} %convert_element_type.12, bf16[864,1,512]{2,1,0:T(2,128)(2,1)S(1)} %copy-done.4), kind=kOutput, calls=%fused_computation.19 | convolution fusion | flops 1811939328 | bytes 8617984 | tf_op jit(solution)/shard_map/dot_general | solution.py:52
  346.3 0.0 copy-done.2
  346.4 0.0 copy-done.3
  346.4 2.4 fusion.15
  348.8 1.2 fusion.11
  350.0 0.2 pad_maximum_fusion
  350.2 2.2 copy.52
  352.4 54.2 %all_to_all.36 = bf16[1024,2,512]{2,1,0:T(2,128)(2,1)S(1)} all-to-all(bf16[1024,2,512]{2,1,0:T(2,128)(2,1)S(1)} %copy.52), channel_id=1, replica_groups=mesh['ga'=2,'band'=16] {'band'}, dimensions={0} | all-to-all | bytes 4194304 | tf_op jit(solution)/shard_map/all_to_all | solution.py:67
  406.5 3.6 copy.58
  (2 shorter events, 0.0 us)
Async XLA Ops:
  25.4 8.6 %copy-start = (bf16[864,2,512]{2,1,0:T(2,128)(2,1)S(1)}, bf16[864,2,512]{2,1,0:T(2,128)(2,1)}, u32[]{:S(2)}) copy-start(bf16[864,2,512]{2,1,0:T(2,128)(2,1)} %param.6) | copy-start | bytes 5308420
  25.4 51.6 %all-to-all-start = ((bf16[16,2,32768]{2,1,0:T(2,128)(2,1)}), bf16[16,2,32768]{2,1,0:T(2,128)(2,1)}, u32[]{:S(2)}, u32[]{:S(2)}) async-start(bf16[16,2,32768]{2,1,0:T(2,128)(2,1)} %reshape.39), calls=%async_computation | async-start | bytes 4194304 | tf_op jit(solution)/shard_map/all_to_all | solution.py:62
  34.0 289.4 %all-reduce.2.cloned.1.call-start = ((), (), s32[]{:S(2)}) async-start(), calls=%async_computation.2 | async-start | bytes 18874368 | tf_op jit(solution)/shard_map/psum | solution.py:64
  102.4 2.2 copy-start.1
  127.8 0.8 copy-start.5
  127.8 1.0 copy-start.6
  127.8 1.0 copy-start.7
  335.5 6.2 %copy-start.4 = (bf16[864,1,512]{2,1,0:T(2,128)(2,1)S(1)}, bf16[864,1,512]{2,1,0:T(2,128)(2,1)}, u32[]{:S(2)}) copy-start(bf16[864,1,512]{2,1,0:T(2,128)(2,1)} %get-tuple-element.9) | copy-start | bytes 2654212
  341.7 4.6 %copy-start.2 = (bf16[864,2048]{1,0:T(8,128)(2,1)S(1)}, bf16[864,2048]{1,0:T(8,128)(2,1)}, u32[]{:S(2)}) copy-start(bf16[864,2048]{1,0:T(8,128)(2,1)} %convert_element_type.12) | copy-start | bytes 10616836
  341.7 4.6 %copy-start.3 = (bf16[864,1,512]{2,1,0:T(2,128)(2,1)S(1)}, bf16[864,1,512]{2,1,0:T(2,128)(2,1)}, u32[]{:S(2)}) copy-start(bf16[864,1,512]{2,1,0:T(2,128)(2,1)} %get-tuple-element.10) | copy-start | bytes 2654212
Sparse Core Ops, SparseCore 0:
  127.9 195.3 all-reduce.1
where the time goes:
time: 419 us; the launch traced here: 417 us
  waiting for transfers between devices  232 us (55%)
  local copies, waits for them, and re-layouts  73.2 us (17%)
  blocking collectives  54.2 us (13%)
  matrix products  32 us (8%)
  between operations  13.6 us (3%)
  starting transfers between devices  8.57 us (2%)
    psum x1, waiting for transfers between devices, per_device(): becp = lax.psum(partial_value, ('ga', 'band'))  189 us
    all_to_all x1, blocking collectives, per_device(): lax.all_to_all(result, 'band', split_axis=0, concat_axis=2, tiled=True)  54.2 us
    all_to_all x1, waiting for transfers between devices, per_device(): lax.all_to_all(orbitals, 'band', split_axis=2, concat_axis=0, tiled=True)  42.6 us
    unnamed x22, local copies, waits for them, and re-layouts  28.5 us
    all_to_all x3, local copies, waits for them, and re-layouts, per_device(): lax.all_to_all(orbitals, 'band', split_axis=2, concat_axis=0, tiled=True)  20.1 us
    dot_general x1, matrix products, project_bands(): lax.dot_general(flat_proj, stacked, (((1,), (1,)), ((), ())), preferred_e...  12.5 us
    dot_general x1, matrix products, apply_coupling(): jnp.einsum('aij,ajc->aic', matrices, blocked, precision=lax.Precision.HIG...  12.2 us
    all_to_all x1, starting transfers between devices, per_device(): lax.all_to_all(orbitals, 'band', split_axis=2, concat_axis=0, tiled=True)  8.52 us
  transfers between devices with their start and end apart: 2, of which 2 were waited for; matrix products, arithmetic and copies ran while one was open for 1% of the time, Pallas kernels for 0%

commit v1 on v0

v1 whole, which is shorter than its diff:
```python
import functools

import jax
import jax.numpy as jnp
from jax import lax
from jax.experimental import pallas as pl
from jax.experimental.pallas import tpu as pltpu
from jax.sharding import PartitionSpec as P

MESH = pl.DeviceIdType.MESH
INNER = 4
F32 = jnp.float32
BF16 = jnp.bfloat16


def coupling_matrix(coupling, species, offsets, total_proj):
    kinds, per_atom = coupling.shape[0], coupling.shape[1]
    column = jnp.arange(total_proj, dtype=jnp.int32)
    within = column % per_atom
    start = column - within
    kind = jnp.sum(
        jnp.where(offsets[:, None] == start[None, :], species[:, None], 0), axis=0
    )
    pick = (jnp.arange(kinds * per_atom, dtype=jnp.int32)[:, None] == (kind * per_atom + within)[None, :])
    table = jnp.transpose(coupling, (2, 0, 1)).reshape(per_atom, kinds * per_atom)
    rows = jnp.dot(table, pick.astype(F32), precision=lax.Precision.HIGHEST, preferred_element_type=F32)
    spread = (within[:, None] == jnp.arange(per_atom, dtype=jnp.int32)[None, :]).astype(F32)
    full = jnp.dot(spread, rows, precision=lax.Precision.HIGHEST, preferred_element_type=F32)
    return jnp.where(start[:, None] == start[None, :], full, 0.0)


def dot_t(a, b):
    return lax.dot_general(a, b, (((1,), (1,)), ((), ())), preferred_element_type=F32)


def dot(a, b):
    return lax.dot_general(a, b, (((1,), (0,)), ((), ())), preferred_element_type=F32)


def kernel(
    outer, groups, o_ref, p_ref, m_ref, out_ref,
    obuf, pbuf, acc, gsend, grecv, zsend, zrecv, dbuf, rbuf,
    o_send, o_recv, p_send, p_recv, l_sem, g_send, g_recv, z_send, z_recv,
    d_send, d_recv, f_send, f_recv, r_send, r_recv, q_sem,
):
    g = lax.axis_index("ga")
    me = lax.axis_index("band")
    o = me // INNER
    n = me % INNER
    bands = o_ref.shape[1]
    wide = p_ref.shape[2]
    span = INNER * wide
    rows = bands // groups
    other = 1 - g
    n1 = n + 1 - 2 * (n % 2)
    n2 = n + 2 - 4 * (n // 2)
    n3 = 3 - n

    def peer(d):
        return (o + d) % outer

    def at_outer(d):
        return {"band": peer(d) * INNER + n}

    side_x = {"band": o * INNER + n1}
    side_y = {"band": o * INNER + n2}
    twin = {"ga": other}

    barrier = pltpu.get_barrier_semaphore()
    partners = [at_outer(d) for d in range(1, outer)] + [side_x, side_y, twin]
    for partner in partners:
        pl.semaphore_signal(barrier, inc=1, device_id=partner, device_id_type=MESH)
    pl.semaphore_wait(barrier, len(partners))

    def remote(src, dst, send, recv, to):
        return pltpu.make_async_remote_copy(
            src_ref=src, dst_ref=dst, send_sem=send, recv_sem=recv, device_id=to, device_id_type=MESH
        )

    mine = pl.ds(pl.multiple_of(o * bands, bands), bands)
    o_copies = []
    for d in range(1, outer):
        src = o_ref.at[:, :, pl.ds(pl.multiple_of(peer(d) * span, span), span)]
        o_copies.append(remote(src, obuf.at[:, mine, :], o_send.at[d], o_recv.at[d], at_outer(d)))
    px = [remote(p_ref.at[c], pbuf.at[n, c], p_send.at[c], p_recv.at[c], side_x) for c in range(2)]
    py = [remote(p_ref.at[c], pbuf.at[n, c], p_send.at[2 + c], p_recv.at[2 + c], side_y) for c in range(2)]
    px[0].start()
    py[1].start()
    for copy in o_copies:
        copy.start()
    px[1].start()
    py[0].start()
    local_o = pltpu.make_async_copy(
        o_ref.at[:, :, pl.ds(pl.multiple_of(o * span, span), span)], obuf.at[:, mine, :], l_sem.at[0]
    )
    local_p = pltpu.make_async_copy(p_ref, pbuf.at[n], l_sem.at[1])
    local_o.start()
    local_p.start()

    px[0].wait_recv()
    fy = remote(pbuf.at[n1, 0], pbuf.at[n1, 0], p_send.at[4], p_recv.at[4], side_y)
    fy.start()
    py[1].wait_recv()
    fx = remote(pbuf.at[n2, 1], pbuf.at[n2, 1], p_send.at[5], p_recv.at[5], side_x)
    fx.start()
    local_o.wait()
    local_p.wait()
    px[1].wait_recv()
    py[0].wait_recv()
    for copy in o_copies:
        copy.wait_recv()

    def project(k, carry):
        slot = jnp.where(k == 0, n, jnp.where(k == 1, n1, jnp.where(k == 2, n2, n3)))
        cols = pl.ds(pl.multiple_of(slot * wide, wide), wide)
        o_real, o_imag = obuf[0, :, cols], obuf[1, :, cols]
        p_real, p_imag = pbuf[slot, 0], pbuf[slot, 1]
        acc[0] += dot_t(o_real, p_real) + dot_t(o_imag, p_imag)
        acc[1] += dot_t(o_imag, p_real) - dot_t(o_real, p_imag)
        return carry

    acc[...] = jnp.zeros_like(acc)
    lax.fori_loop(0, INNER - 1, project, 0)
    fy.wait_recv()
    fx.wait_recv()
    lax.fori_loop(INNER - 1, INNER, project, 0)

    def piece(position, core):
        return pl.ds(pl.multiple_of(position * bands + core * rows, rows), rows)

    order = list(range(1, outer)) + [0]
    g_copies = {}
    for d in order:
        gsend[d] = acc[:, piece(peer(d), other), :].astype(BF16)
        g_copies[d] = remote(gsend.at[d], grecv.at[d], g_send.at[d], g_recv.at[d], twin)
        g_copies[d].start()
    z_copies = {}
    for d in order:
        g_copies[d].wait_recv()
        if d:
            zsend[d] = (acc[:, piece(peer(d), g), :] + grecv[d].astype(F32)).astype(BF16)
            z_copies[d] = remote(zsend.at[d], zrecv.at[d], z_send.at[d], z_recv.at[d], at_outer(d))
            z_copies[d].start()
    total = acc[:, piece(o, g), :] + grecv[0].astype(F32)
    for d in range(1, outer):
        z_copies[d].wait_recv()
        total = total + zrecv[d].astype(F32)

    for c in range(2):
        coupled = lax.dot_general(
            total[c], m_ref[...], (((1,), (0,)), ((), ())),
            precision=lax.Precision.HIGHEST, preferred_element_type=F32,
        )
        dbuf[c, piece(o, g), :] = coupled.astype(BF16)

    own = dbuf.at[:, piece(o, g), :]
    d_copies = {}
    for d in range(1, outer):
        d_copies[d] = remote(own, own, d_send.at[d], d_recv.at[d], at_outer(d))
        d_copies[d].start()
    f_copies = [remote(own, own, f_send.at[0], f_recv.at[0], twin)]
    f_copies[0].start()
    for d in range(1, outer):
        d_copies[d].wait_recv()
        got = dbuf.at[:, piece(peer(outer - d), g), :]
        f_copies.append(remote(got, got, f_send.at[d], f_recv.at[d], twin))
        f_copies[d].start()
    for copy in f_copies:
        copy.wait_recv()

    def back(k, d):
        cols = pl.ds(pl.multiple_of((o * INNER + k) * wide, wide), wide)
        src = rbuf.at[k, :, pl.ds(pl.multiple_of(peer(d) * bands, bands), bands), :]
        if d == 0:
            return pltpu.make_async_copy(src, out_ref.at[:, :, cols], q_sem.at[k])
        return remote(src, out_ref.at[:, :, cols], r_send.at[k, d], r_recv.at[k, d], at_outer(d))

    def add_back(k, carry):
        d_real, d_imag = dbuf[0], dbuf[1]
        p_real, p_imag = pbuf[k, 0], pbuf[k, 1]
        rbuf[k, 0] = (dot(d_real, p_real) - dot(d_imag, p_imag)).astype(BF16)
        rbuf[k, 1] = (dot(d_real, p_imag) + dot(d_imag, p_real)).astype(BF16)
        for d in order:
            back(k, d).start()
        return carry

    lax.fori_loop(0, INNER, add_back, 0)

    for copy in o_copies + px + py + [fx, fy] + list(g_copies.values()) + list(z_copies.values()):
        copy.wait_send()
    for copy in list(d_copies.values()) + f_copies:
        copy.wait_send()

    def finish(k, carry):
        for d in order:
            back(k, d).wait()
        return carry

    lax.fori_loop(0, INNER, finish, 0)


def fused(outer, groups, orbitals, projectors, matrix):
    _, bands, reach = orbitals.shape
    _, total_proj, wide = projectors.shape
    rows = bands // groups
    height = outer * bands
    dma = pltpu.SemaphoreType.DMA
    hbm = pl.BlockSpec(memory_space=pl.ANY)
    flops = 16 * height * total_proj * INNER * wide
    return pl.pallas_call(
        functools.partial(kernel, outer, groups),
        out_shape=jax.ShapeDtypeStruct((2, bands, reach), BF16),
        in_specs=[hbm, hbm, pl.BlockSpec(memory_space=pltpu.VMEM)],
        out_specs=hbm,
        scratch_shapes=[
            pltpu.VMEM((2, height, INNER * wide), BF16),
            pltpu.VMEM((INNER, 2, total_proj, wide), BF16),
            pltpu.VMEM((2, height, total_proj), F32),
            pltpu.VMEM((outer, 2, rows, total_proj), BF16),
            pltpu.VMEM((outer, 2, rows, total_proj), BF16),
            pltpu.VMEM((outer, 2, rows, total_proj), BF16),
            pltpu.VMEM((outer, 2, rows, total_proj), BF16),
            pltpu.VMEM((2, height, total_proj), BF16),
            pltpu.VMEM((INNER, 2, height, wide), BF16),
            dma((outer,)), dma((outer,)), dma((6,)), dma((6,)), dma((2,)),
            dma((outer,)), dma((outer,)), dma((outer,)), dma((outer,)),
            dma((outer,)), dma((outer,)), dma((outer,)), dma((outer,)),
            dma((INNER, outer)), dma((INNER, outer)), dma((INNER,)),
        ],
        compiler_params=pltpu.CompilerParams(
            collective_id=0, has_side_effects=True, vmem_limit_bytes=56 * 1024 * 1024
        ),
        cost_estimate=pl.CostEstimate(flops=flops, bytes_accessed=4 * bands * reach, transcendentals=0),
    )(orbitals, projectors, matrix)


def per_device_kernel(outer, groups, orbitals, projectors, coupling, species, offsets):
    matrix = coupling_matrix(coupling, species, offsets, projectors.shape[0])
    result = fused(
        outer, groups, jnp.transpose(orbitals, (1, 0, 2)), jnp.transpose(projectors, (1, 0, 2)), matrix
    )
    return jnp.transpose(result, (1, 0, 2))


def per_device_plain(orbitals, projectors, coupling, species, offsets):
    total_proj = projectors.shape[0]
    p_real, p_imag = projectors[:, 0, :], projectors[:, 1, :]
    matrix = coupling_matrix(coupling, species, offsets, total_proj)
    spread = lax.all_to_all(orbitals, "band", split_axis=2, concat_axis=0, tiled=True)
    o_real, o_imag = spread[:, 0, :], spread[:, 1, :]
    partial_sum = jnp.stack(
        [dot_t(o_real, p_real) + dot_t(o_imag, p_imag), dot_t(o_imag, p_real) - dot_t(o_real, p_imag)], axis=1
    )
    becp = lax.psum_scatter(partial_sum, ("ga", "band"), scatter_dimension=0, tiled=True)
    coupled = jnp.einsum("bcp,pq->bcq", becp, matrix, precision=lax.Precision.HIGHEST).astype(BF16)
    dbecp = lax.all_gather(coupled, ("ga", "band"), axis=0, tiled=True)
    d_real, d_imag = dbecp[:, 0, :], dbecp[:, 1, :]
    result = jnp.stack(
        [dot(d_real, p_real) - dot(d_imag, p_imag), dot(d_real, p_imag) + dot(d_imag, p_real)], axis=1
    ).astype(BF16)
    return lax.all_to_all(result, "band", split_axis=0, concat_axis=2, tiled=True)


def solution(mesh):
    groups, members = mesh.shape["ga"], mesh.shape["band"]
    if groups == 2 and members % INNER == 0:
        body = functools.partial(per_device_kernel, members // INNER, groups)
    else:
        body = per_device_plain
    placed = (P("band", None, "ga"), P(None, None, ("ga", "band")), P(), P(), P())
    return jax.shard_map(body, mesh=mesh, in_specs=placed, out_specs=P("band", None, "ga"), check_vma=False)
```

time: 419 us -> 157 us (0.37)
  waiting for transfers between devices: 232 us -> 0 us
  Pallas kernels: 0 us -> 140 us
  local copies, waits for them, and re-layouts: 73.2 us -> 11.6 us
  blocking collectives: 54.2 us -> 0 us
  matrix products: 32 us -> 3.33 us
  between operations: 13.6 us -> 0.03 us
  starting transfers between devices: 8.57 us -> 0 us
    psum x1 -> x0, waiting for transfers between devices: 189 us -> none  [per_device(): becp = lax.psum(partial_value, ('ga', 'band'))]
    pallas_call x0 -> x1, Pallas kernels: none -> 140 us  [fused(): pl.pallas_call(functools.partial(kernel, outer, groups), out_shape=jax.Sh...]
    all_to_all x1 -> x0, blocking collectives: 54.2 us -> none  [per_device(): lax.all_to_all(result, 'band', split_axis=0, concat_axis=2, tiled=True)]
    all_to_all x1 -> x0, waiting for transfers between devices: 42.6 us -> none  [per_device(): lax.all_to_all(orbitals, 'band', split_axis=2, concat_axis=0, tiled=True)]
    dot_general x5 -> x2, matrix products: 32 us -> 3.33 us  [the longest x1 3.12 us: coupling_matrix(): jnp.dot(spread, rows, precision=lax.Precision.HIGHEST, preferred_element_...]
    all_to_all x4 -> x0, local copies, waits for them, and re-layouts: 23.8 us -> none  [the longest x3 20.1 us: per_device(): lax.all_to_all(orbitals, 'band', split_axis=2, concat_axis=0, tiled=True)]
    unnamed x22 -> x4, local copies, waits for them, and re-layouts: 28.5 us -> 5.54 us
    all_to_all x1 -> x0, starting transfers between devices: 8.52 us -> none  [per_device(): lax.all_to_all(orbitals, 'band', split_axis=2, concat_axis=0, tiled=True)]
  transfers between devices with their start and end apart: 2 -> 0, of which waited for: 2 -> 0; matrix products, arithmetic and copies ran while one was open for 1% -> 0% of each run, Pallas kernels for 0% -> 0%
where the time goes in v1:
time: 157 us; the launch traced here: 156 us
  Pallas kernels  140 us (89%)
  local copies, waits for them, and re-layouts  11.6 us (7%)
  matrix products  3.33 us (2%)
    pallas_call x1, Pallas kernels, fused(): pl.pallas_call(functools.partial(kernel, outer, groups), out_shape=jax.Sh...  140 us
    unnamed x4, local copies, waits for them, and re-layouts  5.54 us
    transpose x1, local copies, waits for them, and re-layouts, per_device_kernel(): return jnp.transpose(result, (1, 0, 2))  5.08 us

profile of v1, /device:TPU:0, one launch (start us, length us, event | category | flops | bytes accessed | tf_op | source)
XLA Modules:
  0.0 155.7 jit_solution(17634279823967785436)
XLA Ops:
  0.0 0.0 copy-start
  0.0 0.9 select_reduce_fusion
  0.9 0.9 copy.15
  1.8 0.1 reshape.35
  1.9 0.2 fusion
  2.1 3.0 %copy.20 = bf16[864,2,512]{2,0,1:T(8,128)(2,1)} copy(bf16[864,2,512]{2,1,0:T(2,128)(2,1)} %param.6) | data formatting | bytes 3538944 | tf_op args[1]
  5.2 0.0 copy-done
  5.2 2.5 %copy.19 = bf16[64,2,8192]{2,0,1:T(8,128)(2,1)} copy(bf16[64,2,8192]{2,1,0:T(2,128)(2,1)S(1)} %copy-done) | data formatting | bytes 4194304 | tf_op args[0]
  7.7 3.1 %compare_select_fusion.m_ref = f32[864,864]{1,0:T(8,128)} fusion(f32[864,18]{0,1:T(8,128)S(1)} %fusion, s32[864]{0:T(1024)S(1)} %get-tuple-element.6, s32[864]{0:T(1024)S(1)} %get-tuple-element.5), kind=kOutput, calls=%fused_computation | convolution fusion | flops 162751680 | bytes 3055104 | tf_op jit(solution)/shard_map/dot_general | solution.py:28
  10.8 139.8 %shard_map.55 = bf16[2,64,8192]{2,1,0:T(8,128)(2,1)} custom-call(bf16[2,64,8192]{2,1,0:T(8,128)(2,1)} %bitcast.10, bf16[2,864,512]{2,1,0:T(8,128)(2,1)} %bitcast.12, f32[864,864]{1,0:T(8,128)} %compare_select_fusion.m_ref), custom_call_target="tpu_custom_call" | custom-call | flops 7247757312 | bytes 2097152 | tf_op jit(solution)/shard_map/pallas_call | solution.py:210
  150.6 5.1 %copy.16 = bf16[64,2,8192]{2,1,0:T(2,128)(2,1)} copy(bf16[64,2,8192]{2,0,1:T(8,128)(2,1)} %bitcast.11) | data formatting | bytes 4194304 | tf_op jit(solution)/shard_map/transpose | solution.py:242
  (2 shorter events, 0.0 us)
Async XLA Ops:
  0.0 5.2 %copy-start = (bf16[64,2,8192]{2,1,0:T(2,128)(2,1)S(1)}, bf16[64,2,8192]{2,1,0:T(2,128)(2,1)}, u32[]{:S(2)}) copy-start(bf16[64,2,8192]{2,1,0:T(2,128)(2,1)} %param.5) | copy-start | bytes 6291460

commit v2 on v1

v2 whole, which is shorter than its diff:
```python
import functools

import jax
import jax.numpy as jnp
import numpy as np
from jax import lax
from jax.experimental import pallas as pl
from jax.experimental.pallas import tpu as pltpu
from jax.sharding import PartitionSpec as P

MESH = pl.DeviceIdType.MESH
INNER = 4
F32 = jnp.float32
BF16 = jnp.bfloat16


def coupling_rows(coupling, species, offsets, total_proj):
    kinds, per_atom = coupling.shape[0], coupling.shape[1]
    column = jnp.arange(total_proj, dtype=jnp.int32)
    within = column % per_atom
    start = column - within
    kind = jnp.sum(
        jnp.where(offsets[:, None] == start[None, :], species[:, None], 0), axis=0
    )
    pick = (jnp.arange(kinds * per_atom, dtype=jnp.int32)[:, None] == (kind * per_atom + within)[None, :])
    table = jnp.transpose(coupling, (2, 0, 1)).reshape(per_atom, kinds * per_atom)
    return jnp.dot(table, pick.astype(F32), precision=lax.Precision.HIGHEST, preferred_element_type=F32)


def block_diagonal(rows, spread, start_col, start_row):
    full = lax.dot_general(
        spread, rows, (((1,), (0,)), ((), ())), precision=lax.Precision.HIGHEST, preferred_element_type=F32
    )
    return jnp.where(start_col == start_row, full, 0.0)


def block_maps(count, per_atom):
    index = np.arange(count)
    spread = (index[:, None] % per_atom == np.arange(per_atom)[None, :]).astype(np.float32)
    start = (index // per_atom).astype(np.int32)
    return spread, start[:, None], start[None, :]


def dot_t(a, b):
    return lax.dot_general(a, b, (((1,), (1,)), ((), ())), preferred_element_type=F32)


def dot(a, b):
    return lax.dot_general(a, b, (((1,), (0,)), ((), ())), preferred_element_type=F32)


def kernel(
    outer, groups, o_ref, p_ref, rows_ref, spread_ref, col_ref, row_ref, out_ref,
    obuf, pbuf, acc, gsend, grecv, zsend, zrecv, dbuf, rbuf, mbuf,
    o_send, o_recv, p_send, p_recv, l_sem, g_send, g_recv, z_send, z_recv,
    d_send, d_recv, f_send, f_recv, r_send, r_recv, q_sem,
):
    parts = p_ref.shape[1]
    g = lax.axis_index("ga")
    me = lax.axis_index("band")
    o = me // INNER
    n = me % INNER
    bands = o_ref.shape[1]
    wide = p_ref.shape[3]
    span = INNER * wide
    rows = bands // groups
    other = 1 - g
    n1 = n + 1 - 2 * (n % 2)
    n2 = n + 2 - 4 * (n // 2)
    n3 = 3 - n

    def peer(d):
        return (o + d) % outer

    def at_outer(d):
        return {"band": peer(d) * INNER + n}

    side_x = {"band": o * INNER + n1}
    side_y = {"band": o * INNER + n2}
    twin = {"ga": other}

    barrier = pltpu.get_barrier_semaphore()
    partners = [at_outer(d) for d in range(1, outer)] + [side_x, side_y, twin]
    for partner in partners:
        pl.semaphore_signal(barrier, inc=1, device_id=partner, device_id_type=MESH)
    pl.semaphore_wait(barrier, len(partners))

    def remote(src, dst, send, recv, to):
        return pltpu.make_async_remote_copy(
            src_ref=src, dst_ref=dst, send_sem=send, recv_sem=recv, device_id=to, device_id_type=MESH
        )

    mine = pl.ds(pl.multiple_of(o * bands, bands), bands)
    o_copies = []
    for d in range(1, outer):
        src = o_ref.at[:, :, pl.ds(pl.multiple_of(peer(d) * span, span), span)]
        o_copies.append(remote(src, obuf.at[:, mine, :], o_send.at[d], o_recv.at[d], at_outer(d)))
    px, py, fx, fy = {}, {}, {}, {}

    def p_remote(src, slot, c, h, index, to):
        return remote(src, pbuf.at[slot, h, c], p_send.at[h, index], p_recv.at[h, index], to)

    def send_own(h):
        for c in range(2):
            px[h, c] = p_remote(p_ref.at[c, h], n, c, h, c, side_x)
            py[h, c] = p_remote(p_ref.at[c, h], n, c, h, 2 + c, side_y)
        for copy in (px[h, 0], py[h, 1], px[h, 1], py[h, 0]):
            copy.start()

    send_own(0)
    for copy in o_copies:
        copy.start()
    local = [
        pltpu.make_async_copy(
            o_ref.at[:, :, pl.ds(pl.multiple_of(o * span, span), span)], obuf.at[:, mine, :], l_sem.at[0, 0]
        )
    ]
    for h in range(parts):
        for c in range(2):
            local.append(pltpu.make_async_copy(p_ref.at[c, h], pbuf.at[n, h, c], l_sem.at[1 + h, c]))
    for copy in local:
        copy.start()

    for h in range(parts):
        px[h, 0].wait_recv()
        fy[h] = p_remote(pbuf.at[n1, h, 0], n1, 0, h, 4, side_y)
        fy[h].start()
        py[h, 1].wait_recv()
        fx[h] = p_remote(pbuf.at[n2, h, 1], n2, 1, h, 5, side_x)
        fx[h].start()
        if h < parts - 1:
            send_own(h + 1)
        mbuf[h] = block_diagonal(rows_ref[h], spread_ref[...], col_ref[...], row_ref[...])

    for copy in local:
        copy.wait()
    for copy in o_copies:
        copy.wait_recv()

    def project(h):
        def step(slot, carry):
            cols = pl.ds(pl.multiple_of(slot * wide, wide), wide)
            o_real, o_imag = obuf[0, :, cols], obuf[1, :, cols]
            p_real, p_imag = pbuf[slot, h, 0], pbuf[slot, h, 1]
            acc[h, 0] += dot_t(o_real, p_real) + dot_t(o_imag, p_imag)
            acc[h, 1] += dot_t(o_imag, p_real) - dot_t(o_real, p_imag)
            return carry

        px[h, 1].wait_recv()
        py[h, 0].wait_recv()
        fy[h].wait_recv()
        fx[h].wait_recv()
        acc[h] = jnp.zeros_like(acc[h])
        lax.fori_loop(0, INNER, step, 0)

    def piece(position, core):
        return pl.ds(pl.multiple_of(position * bands + core * rows, rows), rows)

    order = list(range(1, outer)) + [0]
    g_copies, z_copies, d_copies, f_copies = {}, {}, {}, {}

    def to_twin(h):
        for d in order:
            gsend[h, d] = acc[h, :, piece(peer(d), other), :]
            g_copies[h, d] = remote(gsend.at[h, d], grecv.at[h, d], g_send.at[h, d], g_recv.at[h, d], twin)
            g_copies[h, d].start()

    def to_outer(h):
        for d in order:
            g_copies[h, d].wait_recv()
            if d:
                zsend[h, d] = (acc[h, :, piece(peer(d), g), :] + grecv[h, d]).astype(BF16)
                z_copies[h, d] = remote(
                    zsend.at[h, d], zrecv.at[h, d], z_send.at[h, d], z_recv.at[h, d], at_outer(d)
                )
                z_copies[h, d].start()

    def couple(h):
        total = acc[h, :, piece(o, g), :] + grecv[h, 0]
        for d in range(1, outer):
            z_copies[h, d].wait_recv()
            total = total + zrecv[h, d].astype(F32)
        for c in range(2):
            coupled = lax.dot_general(
                total[c], mbuf[h], (((1,), (0,)), ((), ())),
                precision=lax.Precision.HIGHEST, preferred_element_type=F32,
            )
            dbuf[h, c, piece(o, g), :] = coupled.astype(BF16)
        own = dbuf.at[h, :, piece(o, g), :]
        for d in range(1, outer):
            d_copies[h, d] = remote(own, own, d_send.at[h, d], d_recv.at[h, d], at_outer(d))
            d_copies[h, d].start()
        f_copies[h, 0] = remote(own, own, f_send.at[h, 0], f_recv.at[h, 0], twin)
        f_copies[h, 0].start()

    def hand_on(h):
        for d in range(1, outer):
            d_copies[h, d].wait_recv()
            got = dbuf.at[h, :, piece(peer(outer - d), g), :]
            f_copies[h, d] = remote(got, got, f_send.at[h, d], f_recv.at[h, d], twin)
            f_copies[h, d].start()

    for h in range(parts - 1):
        project(h)
        to_twin(h)
    for h in range(parts - 1):
        to_outer(h)
    project(parts - 1)
    to_twin(parts - 1)
    to_outer(parts - 1)
    for h in range(parts):
        couple(h)
    for h in range(parts):
        hand_on(h)
    for copy in f_copies.values():
        copy.wait_recv()

    def back(k, d):
        cols = pl.ds(pl.multiple_of((o * INNER + k) * wide, wide), wide)
        src = rbuf.at[k, :, pl.ds(pl.multiple_of(peer(d) * bands, bands), bands), :]
        if d == 0:
            return pltpu.make_async_copy(src, out_ref.at[:, :, cols], q_sem.at[k])
        return remote(src, out_ref.at[:, :, cols], r_send.at[k, d], r_recv.at[k, d], at_outer(d))

    def add_back(k, carry):
        real = imag = 0.0
        for h in range(parts):
            d_real, d_imag = dbuf[h, 0], dbuf[h, 1]
            p_real, p_imag = pbuf[k, h, 0], pbuf[k, h, 1]
            real += dot(d_real, p_real) - dot(d_imag, p_imag)
            imag += dot(d_real, p_imag) + dot(d_imag, p_real)
        rbuf[k, 0] = real.astype(BF16)
        rbuf[k, 1] = imag.astype(BF16)
        for d in order:
            back(k, d).start()
        return carry

    lax.fori_loop(0, INNER, add_back, 0)

    for copy in o_copies:
        copy.wait_send()
    for copies in (px, py, fx, fy, g_copies, z_copies, d_copies, f_copies):
        for copy in copies.values():
            copy.wait_send()

    def finish(k, carry):
        for d in order:
            back(k, d).wait()
        return carry

    lax.fori_loop(0, INNER, finish, 0)


def fused(outer, groups, parts, orbitals, projectors, rows, maps):
    _, bands, reach = orbitals.shape
    _, _, part, wide = projectors.shape
    height = outer * bands
    piece = (parts, outer, 2, bands // groups, part)
    dma = pltpu.SemaphoreType.DMA
    hbm = pl.BlockSpec(memory_space=pl.ANY)
    flops = 16 * height * parts * part * INNER * wide
    return pl.pallas_call(
        functools.partial(kernel, outer, groups),
        out_shape=jax.ShapeDtypeStruct((2, bands, reach), BF16),
        in_specs=[hbm, hbm] + [pl.BlockSpec(memory_space=pltpu.VMEM)] * 4,
        out_specs=hbm,
        scratch_shapes=[
            pltpu.VMEM((2, height, INNER * wide), BF16),
            pltpu.VMEM((INNER, parts, 2, part, wide), BF16),
            pltpu.VMEM((parts, 2, height, part), F32),
            pltpu.VMEM(piece, F32),
            pltpu.VMEM(piece, F32),
            pltpu.VMEM(piece, BF16),
            pltpu.VMEM(piece, BF16),
            pltpu.VMEM((parts, 2, height, part), BF16),
            pltpu.VMEM((INNER, 2, height, wide), BF16),
            pltpu.VMEM((parts, part, part), F32),
            dma((outer,)), dma((outer,)), dma((parts, 6)), dma((parts, 6)), dma((1 + parts, 2)),
        ] + [dma((parts, outer))] * 8 + [
            dma((INNER, outer)), dma((INNER, outer)), dma((INNER,)),
        ],
        compiler_params=pltpu.CompilerParams(
            collective_id=0, has_side_effects=True, vmem_limit_bytes=56 * 1024 * 1024
        ),
        cost_estimate=pl.CostEstimate(flops=flops, bytes_accessed=4 * bands * reach, transcendentals=0),
    )(orbitals, projectors, rows, *maps)


def count_parts(total_proj, per_atom):
    for parts in (3, 2):
        if total_proj % (parts * per_atom) == 0 and total_proj % (parts * 16) == 0:
            return parts
    return 1


def per_device_kernel(outer, groups, orbitals, projectors, coupling, species, offsets):
    total_proj, _, wide = projectors.shape
    per_atom = coupling.shape[1]
    parts = count_parts(total_proj, per_atom)
    part = total_proj // parts
    rows = coupling_rows(coupling, species, offsets, total_proj)
    rows = jnp.transpose(rows.reshape(per_atom, parts, part), (1, 0, 2))
    maps = [jnp.asarray(m) for m in block_maps(part, per_atom)]
    turned = jnp.transpose(projectors, (1, 0, 2)).reshape(2, parts, part, wide)
    result = fused(outer, groups, parts, jnp.transpose(orbitals, (1, 0, 2)), turned, rows, maps)
    return jnp.transpose(result, (1, 0, 2))


def per_device_plain(orbitals, projectors, coupling, species, offsets):
    total_proj = projectors.shape[0]
    p_real, p_imag = projectors[:, 0, :], projectors[:, 1, :]
    rows = coupling_rows(coupling, species, offsets, total_proj)
    matrix = block_diagonal(rows, *block_maps(total_proj, coupling.shape[1]))
    spread = lax.all_to_all(orbitals, "band", split_axis=2, concat_axis=0, tiled=True)
    o_real, o_imag = spread[:, 0, :], spread[:, 1, :]
    partial_sum = jnp.stack(
        [dot_t(o_real, p_real) + dot_t(o_imag, p_imag), dot_t(o_imag, p_real) - dot_t(o_real, p_imag)], axis=1
    )
    becp = lax.psum_scatter(partial_sum, ("ga", "band"), scatter_dimension=0, tiled=True)
    coupled = jnp.einsum("bcp,pq->bcq", becp, matrix, precision=lax.Precision.HIGHEST).astype(BF16)
    dbecp = lax.all_gather(coupled, ("ga", "band"), axis=0, tiled=True)
    d_real, d_imag = dbecp[:, 0, :], dbecp[:, 1, :]
    result = jnp.stack(
        [dot(d_real, p_real) - dot(d_imag, p_imag), dot(d_real, p_imag) + dot(d_imag, p_real)], axis=1
    ).astype(BF16)
    return lax.all_to_all(result, "band", split_axis=0, concat_axis=2, tiled=True)


def solution(mesh):
    groups, members = mesh.shape["ga"], mesh.shape["band"]
    if groups == 2 and members % INNER == 0:
        body = functools.partial(per_device_kernel, members // INNER, groups)
    else:
        body = per_device_plain
    placed = (P("band", None, "ga"), P(None, None, ("ga", "band")), P(), P(), P())
    return jax.shard_map(body, mesh=mesh, in_specs=placed, out_specs=P("band", None, "ga"), check_vma=False)
```

time: 157 us -> 150 us (0.955)
  Pallas kernels: 140 us -> 136 us
  matrix products: 3.33 us -> 0.21 us
    pallas_call x1, Pallas kernels: 140 us -> 136 us  [fused(): pl.pallas_call(functools.partial(kernel, outer, groups), out_shape=jax.Sh...]
    transpose x1 -> x2, local copies, waits for them, and re-layouts: 0.88 us -> 4 us  [the longest x1 2.98 us: per_device_kernel(): turned = jnp.transpose(projectors, (1, 0, 2)).reshape(2, parts, part, wide)]
    dot_general x2 -> x1, matrix products: 3.33 us -> 0.21 us  [coupling_rows(): jnp.dot(table, pick.astype(F32), precision=lax.Precision.HIGHEST, preferr...]
    unnamed x4 -> x3, local copies, waits for them, and re-layouts: 5.54 us -> 2.49 us
where the time goes in v2:
time: 150 us; the launch traced here: 149 us
  Pallas kernels  136 us (91%)
  local copies, waits for them, and re-layouts  12.4 us (8%)
    pallas_call x1, Pallas kernels, fused(): pl.pallas_call(functools.partial(kernel, outer, groups), out_shape=jax.Sh...  136 us
    transpose x1, local copies, waits for them, and re-layouts, per_device_kernel(): return jnp.transpose(result, (1, 0, 2))  5.08 us

profile of v2, /device:TPU:0, one launch (start us, length us, event | category | flops | bytes accessed | tf_op | source)
XLA Modules:
  0.0 149.3 jit_solution(10535930566441425135)
XLA Ops:
  0.0 0.8 select_reduce_fusion
  0.8 0.0 copy-start
  0.8 1.0 copy.19
  1.8 0.1 reshape.29
  1.9 0.2 convolution_bitcast_fusion
  2.1 0.1 reshape.30
  2.2 0.7 copy.25
  2.9 3.0 %copy.18 = bf16[2,864,512]{2,1,0:T(8,128)(2,1)} copy(bf16[2,864,512]{2,0,1:T(2,128)(2,1)} %bitcast.15) | data formatting | bytes 3538944 | tf_op jit(solution)/shard_map/transpose | solution.py:304
  5.9 0.0 copy-done
  5.9 2.5 %copy.24 = bf16[64,2,8192]{2,0,1:T(8,128)(2,1)} copy(bf16[64,2,8192]{2,1,0:T(2,128)(2,1)S(1)} %copy-done) | data formatting | bytes 4194304 | tf_op args[0]
  8.4 135.9 %shard_map.82 = bf16[2,64,8192]{2,1,0:T(8,128)(2,1)} custom-call(bf16[2,64,8192]{2,1,0:T(8,128)(2,1)} %bitcast.14, bf16[2,3,288,512]{3,2,1,0:T(8,128)(2,1)} %bitcast.16, f32[3,18,288]{2,1,0:T(8,128)} %bitcast.17, f32[288,18]{1,0:T(8,128)} %constant.20.clone.spread_ref, s32[288,1]{1,0:T(8,128)} %constant.21.clone.col_ref, s32[1,288]{1,0:T(1,128)} %constant.22.clone.row_ref), custom_call_target="tpu_custom_call" | custom-call | flops 7247757312 | bytes 2097152 | tf_op jit(solution)/shard_map/pallas_call | solution.py:262
  144.2 5.1 %copy.21 = bf16[64,2,8192]{2,1,0:T(2,128)(2,1)} copy(bf16[64,2,8192]{2,0,1:T(8,128)(2,1)} %bitcast.13) | data formatting | bytes 4194304 | tf_op jit(solution)/shard_map/transpose | solution.py:306
  (2 shorter events, 0.0 us)
Async XLA Ops:
  0.8 5.1 %copy-start = (bf16[64,2,8192]{2,1,0:T(2,128)(2,1)S(1)}, bf16[64,2,8192]{2,1,0:T(2,128)(2,1)}, u32[]{:S(2)}) copy-start(bf16[64,2,8192]{2,1,0:T(2,128)(2,1)} %param.8) | copy-start | bytes 6291460

commit v3 on v2

--- a/solution.py
+++ b/solution.py
@@ -280,7 +280,7 @@
             dma((INNER, outer)), dma((INNER, outer)), dma((INNER,)),
         ],
         compiler_params=pltpu.CompilerParams(
-            collective_id=0, has_side_effects=True, vmem_limit_bytes=56 * 1024 * 1024
+            collective_id=0, has_side_effects=True, vmem_limit_bytes=32 * 1024 * 1024
         ),
         cost_estimate=pl.CostEstimate(flops=flops, bytes_accessed=4 * bands * reach, transcendentals=0),
     )(orbitals, projectors, rows, *maps)

time: 150 us -> 144 us (0.960)
  local copies, waits for them, and re-layouts: 12.4 us -> 7.67 us
    transpose x1, local copies, waits for them, and re-layouts: 5.08 us -> 3.49 us  [per_device_kernel(): return jnp.transpose(result, (1, 0, 2))]
where the time goes in v3:
time: 144 us; the launch traced here: 143 us
  Pallas kernels  135 us (94%)
  local copies, waits for them, and re-layouts  7.67 us (5%)
    pallas_call x1, Pallas kernels, fused(): pl.pallas_call(functools.partial(kernel, outer, groups), out_shape=jax.Sh...  135 us
    transpose x1, local copies, waits for them, and re-layouts, per_device_kernel(): return jnp.transpose(result, (1, 0, 2))  3.49 us

profile of v3, /device:TPU:0, one launch (start us, length us, event | category | flops | bytes accessed | tf_op | source)
XLA Modules:
  0.0 143.4 jit_solution(79314996359445342)
XLA Ops:
  0.0 0.8 select_reduce_fusion
  0.8 0.0 copy-start.3
  0.8 1.0 copy.19
  1.8 0.1 reshape.29
  1.9 0.2 convolution_bitcast_fusion
  2.1 0.1 reshape.30
  2.3 1.8 %copy.18 = bf16[2,864,512]{2,1,0:T(8,128)(2,1)S(1)} copy(bf16[2,864,512]{2,0,1:T(2,128)(2,1)} %bitcast.17) | data formatting | bytes 3538944 | tf_op jit(solution)/shard_map/transpose | solution.py:304
  4.0 0.0 copy-done.3
  4.0 0.0 copy-start
  4.1 0.0 copy-start.1
  4.1 0.0 copy-start.2
  4.1 1.2 copy.24
  5.2 0.0 copy-done
  5.3 0.0 copy-done.1
  5.3 0.0 copy-done.2
  5.3 134.6 %shard_map.82 = bf16[2,64,8192]{2,1,0:T(8,128)(2,1)S(1)} custom-call(bf16[2,64,8192]{2,1,0:T(8,128)(2,1)S(1)} %bitcast.14, bf16[2,3,288,512]{3,2,1,0:T(8,128)(2,1)S(1)} %bitcast.15, f32[3,18,288]{2,1,0:T(8,128)S(1)} %bitcast.16, f32[288,18]{1,0:T(8,128)S(1)} %copy-done.1, s32[288,1]{1,0:T(8,128)S(1)} %copy-done, s32[1,288]{1,0:T(1,128)S(1)} %copy-done.2), custom_call_target="tpu_custom_call" | custom-call | flops 7247757312 | bytes 2097152 | tf_op jit(solution)/shard_map/pallas_call | solution.py:262
  139.9 3.5 %copy.21 = bf16[64,2,8192]{2,1,0:T(2,128)(2,1)} copy(bf16[64,2,8192]{2,0,1:T(8,128)(2,1)S(1)} %bitcast.13) | data formatting | bytes 4194304 | tf_op jit(solution)/shard_map/transpose | solution.py:306
  (3 shorter events, 0.0 us)
Async XLA Ops:
  0.8 3.3 %copy-start.3 = (bf16[64,2,8192]{2,1,0:T(2,128)(2,1)S(1)}, bf16[64,2,8192]{2,1,0:T(2,128)(2,1)}, u32[]{:S(2)}) copy-start(bf16[64,2,8192]{2,1,0:T(2,128)(2,1)} %param.8) | copy-start | bytes 6291460
  4.0 1.2 copy-start
  4.1 1.2 copy-start.1
  4.1 1.2 copy-start.2
